TPU v7x, 32 devices: a whole 2x2x4 slice. The times are simulated.
32 devices in a mesh: tensor: 8 (over z, y), dp: 4 (over x, core).
Axes of the slice: x: 2, y: 2, z: 4, core: 2. Of those that a mesh axis runs over, the one named last changes fastest.
Arguments:
- base_weight: bfloat16 [2, 2, 4096, 14336], P(None, None, 'tensor', 'dp'), may hold values from -0.125 to 0.125
- adapter_left: bfloat16 [2, 2, 4096, 16], P(None, None, 'tensor'), may hold values from -0.059814453 to 0.059814453
- adapter_right: bfloat16 [2, 2, 16, 14336], P(None, None, None, 'dp'), may hold values from -1.5 to 1.5
- magnitude: bfloat16 [2, 2, 14336], P(None, None, 'dp'), may hold values from 16 to 256
Outputs:
- merged_weight: bfloat16 [2, 2, 14336, 4096], P(None, None, 'tensor')
All inputs are finite; a program needn't handle non-finite values.
Results may differ from a plain program's by a relative error of at most 0.0004.
Values may be sent and summed in bfloat16 or wider, within the bound.
A program may use at most 384 MiB of HBM per device.

v0:
```python
import functools

import jax
import jax.numpy as jnp
from jax import lax
from jax.experimental import pallas as pl
from jax.experimental.pallas import tpu as pltpu
from jax.sharding import PartitionSpec as P

MESH = pl.DeviceIdType.MESH


def exchange_kernel(sizes, chunks, relayed, s, g, rb, recv, xs, cs, a_send, a_recv, b_send, r_send):
    tensor_count, replica_count = sizes
    group = tensor_count // replica_count
    half_t, half_r = tensor_count // 2, replica_count // 2
    serve = s.shape[3]
    parts = ((0, relayed), (relayed, serve - relayed))
    t, d = lax.axis_index("tensor"), lax.axis_index("dp")
    twin = lax.rem(d + half_r, replica_count)
    mate = d + 1 - 2 * lax.rem(d, 2)
    near = t // half_t == d // half_r
    far = jnp.logical_not(near)
    home = t // group
    is_home, is_twin = home == d, home == twin
    base = (t // half_t) * half_t
    other = half_t - base

    def near_source(i):
        return base + lax.rem(t - base + i, half_t)

    def far_source(i):
        return other + lax.rem(t - base + i, half_t)

    def own(k, j, p):
        return s.at[k, j, :, pl.ds(*parts[p])]

    def slot(ts, k, p):
        return g.at[ts, k, :, pl.ds(*parts[p])]

    def send(src, ts, k, p, sem, tensor, dp):
        return pltpu.make_async_remote_copy(
            src_ref=src, dst_ref=slot(ts, k, p), send_sem=sem, recv_sem=recv.at[ts, k, p],
            device_id={"tensor": tensor, "dp": dp}, device_id_type=MESH,
        )

    def to_twin(src, ts, k, p):
        return send(src, ts, k, p, xs.at[ts, k, p], t, twin)

    def to_mate(src, ts, k, p):
        return send(src, ts, k, p, cs.at[ts, k, p], t, mate)

    def to_relay(k, j):
        return pltpu.make_async_remote_copy(
            src_ref=own(k, j, 0), dst_ref=rb.at[k, j], send_sem=a_send.at[k, j], recv_sem=a_recv.at[k, j],
            device_id={"tensor": t, "dp": twin}, device_id_type=MESH,
        )

    def relay(k, j):
        return send(rb.at[k, j], t, k, 0, r_send.at[k, j], twin * group + j, d)

    def direct(k, j, p):
        return send(own(k, j, p), t, k, p, b_send.at[k, j, p], d * group + j, d)

    def keep(k, p):
        return pltpu.make_async_copy(own(k, lax.rem(t, group), p), slot(t, k, p), recv.at[t, k, p])

    def got(ts, k, p):
        to_mate(slot(ts, k, p), ts, k, p).wait_recv()

    def loop(count, body, first=0):
        lax.fori_loop(first, count, lambda i, c: (body(i), c)[1], 0)

    def each_piece(body):
        loop(chunks, lambda k: loop(group, lambda j: body(k, j)))

    def start_piece(k, j):
        leaves = d * group + j != t

        @pl.when(far)
        def _():
            to_relay(k, j).start()
            direct(k, j, 1).start()

        @pl.when(jnp.logical_and(near, leaves))
        def _():
            direct(k, j, 0).start()
            direct(k, j, 1).start()

        @pl.when(jnp.logical_not(leaves))
        def _():
            for p in range(2):
                src = own(k, j, p)
                to_twin(src, t, k, p).start()
                to_mate(src, t, k, p).start()
                keep(k, p).start()

    each_piece(start_piece)

    def pass_on(ts, k, p):
        got(ts, k, p)
        to_twin(slot(ts, k, p), ts, k, p).start()
        to_mate(slot(ts, k, p), ts, k, p).start()

    def hand_over(ts, k, p):
        got(ts, k, p)
        to_mate(slot(ts, k, p), ts, k, p).start()

    def relay_step(k):
        @pl.when(near)
        def _():
            def one(j):
                to_relay(k, j).wait_recv()
                relay(k, j).start()

            loop(group, one)

    def arrivals(k):
        @pl.when(is_home)
        def _():
            def one(i):
                pass_on(near_source(i), k, 0)
                pass_on(near_source(i), k, 1)

            loop(half_t, one, 1)
            loop(half_t, lambda i: pass_on(far_source(i), k, 1))

        @pl.when(is_twin)
        def _():
            loop(half_t, lambda i: pass_on(far_source(i), k, 0))

    def second_hand(k):
        @pl.when(is_home)
        def _():
            loop(half_t, lambda i: hand_over(far_source(i), k, 0))

        @pl.when(is_twin)
        def _():
            def one(i):
                hand_over(near_source(i), k, 0)
                hand_over(near_source(i), k, 1)

            loop(half_t, one)
            loop(half_t, lambda i: hand_over(far_source(i), k, 1))

    relay_step(0)

    def step(k):
        @pl.when(k + 1 < chunks)
        def _():
            relay_step(k + 1)

        arrivals(k)

        @pl.when(k > 0)
        def _():
            second_hand(k - 1)

    loop(chunks, step)
    second_hand(chunks - 1)

    serving = jnp.logical_or(is_home, is_twin)

    @pl.when(jnp.logical_not(serving))
    def _():
        def one(k, ts):
            got(ts, k, 0)
            got(ts, k, 1)

        loop(chunks, lambda k: loop(tensor_count, lambda ts: one(k, ts)))

    @pl.when(is_home)
    def _():
        def one(k):
            keep(k, 0).wait()
            keep(k, 1).wait()

        loop(chunks, one)

    def finish_piece(k, j):
        leaves = d * group + j != t

        @pl.when(far)
        def _():
            to_relay(k, j).wait_send()
            direct(k, j, 1).wait_send()

        @pl.when(near)
        def _():
            relay(k, j).wait_send()

        @pl.when(jnp.logical_and(near, leaves))
        def _():
            direct(k, j, 0).wait_send()
            direct(k, j, 1).wait_send()

    each_piece(finish_piece)

    @pl.when(serving)
    def _():
        def one(k, ts):
            to_mate(slot(ts, k, 0), ts, k, 0).wait_send()
            to_mate(slot(ts, k, 1), ts, k, 1).wait_send()

        loop(chunks, lambda k: loop(tensor_count, lambda ts: one(k, ts)))

    @pl.when(is_home)
    def _():
        def one(k, i):
            to_twin(slot(near_source(i), k, 0), near_source(i), k, 0).wait_send()
            to_twin(slot(near_source(i), k, 1), near_source(i), k, 1).wait_send()
            to_twin(slot(far_source(i), k, 1), far_source(i), k, 1).wait_send()

        loop(chunks, lambda k: loop(half_t, lambda i: one(k, i)))

    @pl.when(is_twin)
    def _():
        def one(k, i):
            to_twin(slot(far_source(i), k, 0), far_source(i), k, 0).wait_send()

        loop(chunks, lambda k: loop(half_t, lambda i: one(k, i)))


def exchange(s, tensor_count, replica_count, relayed):
    chunks, group, each, serve, rows = s.shape
    dma = pltpu.SemaphoreType.DMA
    g, _ = pl.pallas_call(
        functools.partial(exchange_kernel, (tensor_count, replica_count), chunks, relayed),
        out_shape=(
            jax.ShapeDtypeStruct((tensor_count, chunks, each, serve, rows), s.dtype),
            jax.ShapeDtypeStruct((chunks, group, each, relayed, rows), s.dtype),
        ),
        in_specs=[pl.BlockSpec(memory_space=pl.ANY)],
        out_specs=[pl.BlockSpec(memory_space=pl.ANY)] * 2,
        scratch_shapes=[dma((tensor_count, chunks, 2))] * 3
        + [dma((chunks, group))] * 2
        + [dma((chunks, group, 2)), dma((chunks, group))],
        compiler_params=pltpu.CompilerParams(has_side_effects=True),
    )(s)
    return g


def flip_kernel(w, o):
    o[0] = w[0].T


def flip(w):
    stacks, rows, cols = w.shape
    if rows % 128:
        return w.swapaxes(1, 2)
    wide = next(n for n in (512, 256, 128, cols) if cols % n == 0)
    return pl.pallas_call(
        flip_kernel,
        grid=(stacks, cols // wide),
        in_specs=[pl.BlockSpec((1, rows, wide), lambda e, c: (e, 0, c))],
        out_specs=pl.BlockSpec((1, wide, rows), lambda e, c: (e, c, 0)),
        out_shape=jax.ShapeDtypeStruct((stacks, cols, rows), w.dtype),
    )(w)


def merge_kernel(count, rows, g, left, right, magnitude, o, merged):
    squares = None
    for n in range(count):
        at = slice(n * rows, (n + 1) * rows)
        piece = g[n, 0].astype(jnp.float32) + jnp.dot(
            right[0], left[0, :, at], preferred_element_type=jnp.float32
        )
        merged[:, at] = piece
        total = jnp.sum(piece * piece, axis=1, keepdims=True)
        squares = total if squares is None else squares + total
    scaling = magnitude[0].astype(jnp.float32) / jnp.sqrt(squares + 1e-06)
    for n in range(count):
        at = slice(n * rows, (n + 1) * rows)
        o[0, :, at] = (merged[:, at] * scaling).astype(o.dtype)


def merge(g, left, right, magnitude):
    count, stacks, serve, rows = g.shape
    rank = right.shape[2]
    if rows % 128:
        joined = g.transpose(1, 2, 0, 3).reshape(stacks, serve, count * rows)
        merged = joined.astype(jnp.float32) + jnp.einsum(
            "xfr,xri->xfi", right, left, preferred_element_type=jnp.float32
        )
        squares = jnp.sum(merged * merged, axis=2, keepdims=True)
        scaling = magnitude.astype(jnp.float32) / jnp.sqrt(squares + 1e-06)
        return (merged * scaling).astype(g.dtype)
    tall = next(n for n in (256, 128, 64, 32, 16, serve) if serve % n == 0)
    return pl.pallas_call(
        functools.partial(merge_kernel, count, rows),
        grid=(stacks, serve // tall),
        in_specs=[
            pl.BlockSpec((count, 1, tall, rows), lambda e, f: (0, e, f, 0)),
            pl.BlockSpec((1, rank, count * rows), lambda e, f: (e, 0, 0)),
            pl.BlockSpec((1, tall, rank), lambda e, f: (e, f, 0)),
            pl.BlockSpec((1, tall, 1), lambda e, f: (e, f, 0)),
        ],
        out_specs=pl.BlockSpec((1, tall, count * rows), lambda e, f: (e, f, 0)),
        out_shape=jax.ShapeDtypeStruct((stacks, serve, count * rows), g.dtype),
        scratch_shapes=[pltpu.VMEM((tall, count * rows), jnp.float32)],
    )(g, left, right, magnitude)


def shards(base_weight, adapter_left, adapter_right, magnitude):
    tensor_count = lax.axis_size("tensor")
    replica_count = lax.axis_size("dp")
    experts, projections, rows, cols = base_weight.shape
    rank = adapter_left.shape[3]
    stacks = experts * projections
    group = tensor_count // replica_count
    serve = cols // group
    chunks = stacks if tensor_count <= 16 else 1
    relayed = (2 * (serve // 16) + 1) // 3 * 16

    s = flip(base_weight.reshape(stacks, rows, cols))
    if chunks == 1:
        s = s.reshape(1, stacks, group, serve, rows).swapaxes(1, 2)
    else:
        s = s.reshape(chunks, group, 1, serve, rows)
    g = exchange(s, tensor_count, replica_count, relayed).reshape(tensor_count, stacks, serve, rows)

    left = lax.all_gather(adapter_left.swapaxes(2, 3), "tensor", axis=3, tiled=True)
    right_all = lax.all_gather(adapter_right, "dp", axis=3, tiled=True)
    magnitude_all = lax.all_gather(magnitude, "dp", axis=2, tiled=True)
    start = lax.axis_index("tensor") * serve
    right = lax.dynamic_slice_in_dim(right_all, start, serve, 3).swapaxes(2, 3)
    strength = lax.dynamic_slice_in_dim(magnitude_all, start, serve, 2)
    out = merge(
        g,
        left.reshape(stacks, rank, -1),
        right.reshape(stacks, serve, rank),
        strength.reshape(stacks, serve, 1),
    )
    return out.reshape(experts, projections, serve, -1)


def solution(mesh):
    in_specs = (
        P(None, None, "tensor", "dp"),
        P(None, None, "tensor", None),
        P(None, None, None, "dp"),
        P(None, None, "dp"),
    )
    out_specs = P(None, None, "tensor", None)
    return jax.shard_map(shards, mesh=mesh, in_specs=in_specs, out_specs=out_specs, check_vma=False)
```

profile of v0, /device:TPU:0, one launch (start us, length us, event | category | flops | bytes accessed | tf_op | source)
XLA Modules:
  0.0 660.6 jit_solution(13612785062895768270)
XLA Ops:
  6.5 0.0 all-gather.2.cloned.1.call-start
  6.5 0.7 all-gather.2.cloned.1.call-update
  7.3 6.6 %all_gather.11 = bf16[2,2,14336]{2,1,0:T(2,128)(2,1)S(1)} all-gather(bf16[2,2,3584]{2,1,0:T(2,128)(2,1)} %param.7), channel_id=1, replica_groups=mesh['tensor'=8,'dp'=4] {'dp'}, dimensions={2}, use_global_device_ids=true | all-gather | bytes 143360 | tf_op jit(solution)/shard_map/all_gather | solution.py:324
  13.9 5.1 reshape.28.magnitude
  19.0 21.9 %shard_map.46 = bf16[4,3584,512]{2,1,0:T(8,128)(2,1)} custom-call(bf16[4,512,3584]{2,1,0:T(8,128)(2,1)} %bitcast.11), custom_call_target="tpu_custom_call" | custom-call | tf_op jit(solution)/shard_map/pallas_call | solution.py:252
  41.0 0.0 copy-start
  41.0 495.3 %shard_map.47 = (bf16[8,4,1,1792,512]{4,3,2,1,0:T(8,128)(2,1)}, bf16[4,2,1,1200,512]{4,3,2,1,0:T(8,128)(2,1)}) custom-call(bf16[4,2,1,1792,512]{4,3,2,1,0:T(8,128)(2,1)} %bitcast.9), custom_call_target="tpu_custom_call" | custom-call | tf_op jit(solution)/shard_map/pallas_call | solution.py:227
  536.3 0.0 copy-done
  536.3 56.4 %all_gather.9 = bf16[2,2,16,4096]{3,2,1,0:T(8,128)(2,1)} all-gather(bf16[2,2,16,512]{3,2,1,0:T(8,128)(2,1)S(1)} %bitcast.14), channel_id=1, replica_groups=mesh['tensor'=8,'dp'=4] {'tensor'}, dimensions={3}, use_global_device_ids=true | all-gather | bytes 589824 | tf_op jit(solution)/shard_map/all_gather | solution.py:322
  592.7 0.0 all-gather.2.cloned.1.call-done
  592.7 1.0 dynamic-slice_bitcast_fusion
  593.6 1.6 copy.6
  595.2 58.5 %shard_map.48 = bf16[4,1792,4096]{2,1,0:T(8,128)(2,1)} custom-call(bf16[8,4,1792,512]{3,2,1,0:T(8,128)(2,1)} %bitcast.10, bf16[4,16,4096]{2,1,0:T(8,128)(2,1)} %bitcast.13, bf16[4,1792,16]{2,1,0:T(8,128)(2,1)} %bitcast.12, bf16[4,1792,1]{2,1,0:T(8,128)(2,1)} %reshape.28.magnitude), custom_call_target="tpu_custom_call" | custom-call | tf_op jit(solution)/shard_map/pallas_call | solution.py:289
  (1 shorter events, 0.0 us)
Async XLA Ops:
  6.5 586.1 %all-gather.2.cloned.1.call-start = ((), (), s32[]{:S(2)}) async-start(), calls=%async_computation | async-start | bytes 2293760 | tf_op jit(solution)/shard_map/all_gather | solution.py:323
  41.0 495.3 %copy-start = (bf16[2,2,512,16]{2,3,1,0:T(8,128)(2,1)S(1)}, bf16[2,2,512,16]{2,3,1,0:T(8,128)(2,1)}, u32[]{:S(2)}) copy-start(bf16[2,2,512,16]{2,3,1,0:T(8,128)(2,1)} %param.5) | copy-start | bytes 196612
Sparse Core Ops, SparseCore 0:
  8.9 23.8 all-gather.1
where the time goes:
time: 662 us; the launch traced here: 661 us
  Pallas kernels  576 us (87%)
  blocking collectives  63 us (10%)
  between operations  13.4 us (2%)
  local copies, waits for them, and re-layouts  7.72 us (1%)
    pallas_call x1, Pallas kernels, exchange(): pl.pallas_call(functools.partial(exchange_kernel, (tensor_count, replica_...  495 us
    pallas_call x1, Pallas kernels, merge(): pl.pallas_call(functools.partial(merge_kernel, count, rows), grid=(stacks...  58.5 us
    all_gather x1, blocking collectives, shards(): lax.all_gather(adapter_left.swapaxes(2, 3), 'tensor', axis=3, tiled=True)  56.4 us
    pallas_call x1, Pallas kernels, flip(): pl.pallas_call(flip_kernel, grid=(stacks, cols // wide), in_specs=[pl.Blo...  21.9 us
  transfers between devices with their start and end apart: 1, of which 0 were waited for; matrix products, arithmetic and copies ran while one was open for 1% of the time, Pallas kernels for 78%

commit v1 on v0

--- a/solution.py
+++ b/solution.py
@@ -301,6 +301,436 @@
     )(g, left, right, magnitude)
 
 
+UNIT = 128
+AHEAD, RELAY_AHEAD, MERGE_LAG = 4, 2, 1
+
+
+def fused_kernel(
+    tensor_count, w, lt, r, m, o, s, g, rb, win, left, right, strength, merged, ob,
+    w_sem, s_send, g_recv, rb_recv, rb_send, f_send, l_own, l_recv, l_send, l_mate, l_twin,
+    p_recv, p_send, o_local, o_send, o_recv,
+):
+    units, _, unit, rows = g.shape
+    group = s.shape[1]
+    half_t = tensor_count // 2
+    serve = o.shape[1]
+    half = serve // 2
+    per = half // unit
+    stacks = units // per
+    t, d = lax.axis_index("tensor"), lax.axis_index("dp")
+    x, c = d // 2, lax.rem(d, 2)
+    twin = lax.rem(d + 2, 4)
+    mate = d + 1 - 2 * c
+    near = t // half_t == x
+    far = jnp.logical_not(near)
+    home = t // group == d
+    base = (t // half_t) * half_t
+    other = half_t - base
+
+    def near_source(i):
+        return base + lax.rem(t - base + i, half_t)
+
+    def far_source(i):
+        return other + lax.rem(t - base + i, half_t)
+
+    def loop(count, body, first=0):
+        lax.fori_loop(first, count, lambda i, carry: (body(i), carry)[1], 0)
+
+    def is_direct(v, h):
+        return lax.rem(v + h, 3) == 1
+
+    def direct_before(v, h):
+        return (v + 1 + h) // 3
+
+    def relay_index(v, h):
+        return v - direct_before(v, h)
+
+    def remote(src, dst, send_sem, recv_sem, tensor, dp):
+        return pltpu.make_async_remote_copy(
+            src_ref=src, dst_ref=dst, send_sem=send_sem, recv_sem=recv_sem,
+            device_id={"tensor": tensor, "dp": dp}, device_id_type=MESH,
+        )
+
+    pairs = [(j, h) for j in range(group) for h in range(2)]
+
+    def load(v, j, h):
+        k, q = v // per, lax.rem(v, per)
+        at = pl.multiple_of(j * serve + h * half + q * unit, unit)
+        slot = lax.rem(v, 2)
+        return pltpu.make_async_copy(
+            w.at[k, :, pl.ds(at, unit)], win.at[slot, j, h], w_sem.at[slot, j, h]
+        )
+
+    def start_load(v):
+        for j, h in pairs:
+            load(v, j, h).start()
+
+    def to_server(v, j, h):
+        return remote(
+            s.at[v, j, h], g.at[v, t], s_send.at[v // per, j, h], g_recv.at[v, t],
+            d * group + j, x * 2 + h,
+        )
+
+    def to_relay(v, j, h):
+        at = relay_index(v, h)
+        return remote(
+            s.at[v, j, h], rb.at[at, j, h], s_send.at[v // per, j, h], rb_recv.at[at, j, h], t, twin
+        )
+
+    def stays(j, h):
+        return jnp.logical_and(d * group + j == t, c == h)
+
+    def flip_and_send(v):
+        slot = lax.rem(v, 2)
+        for j, h in pairs:
+            load(v, j, h).wait()
+            turned = win[slot, j, h].T
+            s[v, j, h] = turned
+            own = stays(j, h)
+
+            @pl.when(own)
+            def _():
+                g[v, t] = turned
+
+            by_hand = jnp.logical_and(far, jnp.logical_not(is_direct(v, h)))
+
+            @pl.when(by_hand)
+            def _():
+                to_relay(v, j, h).start()
+
+            @pl.when(jnp.logical_not(jnp.logical_or(own, by_hand)))
+            def _():
+                to_server(v, j, h).start()
+
+        @pl.when(v + 2 < units)
+        def _():
+            start_load(v + 2)
+
+    def relay(v, j, h):
+        return remote(
+            rb.at[relay_index(v, h), j, h], g.at[v, t], rb_send.at[j, h], g_recv.at[v, t],
+            twin * group + j, x * 2 + h,
+        )
+
+    def relay_step(v):
+        for j, h in pairs:
+
+            @pl.when(jnp.logical_and(near, jnp.logical_not(is_direct(v, h))))
+            def _():
+                to_relay(v, j, h).wait_recv()
+                relay(v, j, h).start()
+
+    def forward(v, ts):
+        return remote(g.at[v, ts], g.at[v, ts], f_send.at[ts], g_recv.at[v, ts], t, twin)
+
+    def got(v, ts):
+        forward(v, ts).wait_recv()
+
+    def pass_on(v, ts):
+        got(v, ts)
+        forward(v, ts).start()
+
+    def arrivals(v):
+        @pl.when(near)
+        def _():
+            @pl.when(home)
+            def _():
+                forward(v, t).start()
+
+            @pl.when(jnp.logical_not(home))
+            def _():
+                pass_on(v, t)
+
+            loop(half_t, lambda i: pass_on(v, near_source(i)), 1)
+
+            @pl.when(is_direct(v, c))
+            def _():
+                loop(half_t, lambda i: pass_on(v, far_source(i)))
+
+        @pl.when(jnp.logical_and(far, jnp.logical_not(is_direct(v, c))))
+        def _():
+            loop(half_t, lambda i: pass_on(v, far_source(i)))
+
+    def second_hand(v):
+        @pl.when(far)
+        def _():
+            loop(half_t, lambda i: got(v, near_source(i)))
+
+            @pl.when(is_direct(v, c))
+            def _():
+                loop(half_t, lambda i: got(v, far_source(i)))
+
+        @pl.when(jnp.logical_and(near, jnp.logical_not(is_direct(v, c))))
+        def _():
+            loop(half_t, lambda i: got(v, far_source(i)))
+
+    def out_rows(v, core):
+        k, q = v // per, lax.rem(v, per)
+        return o.at[k, pl.ds(pl.multiple_of(core * half + q * unit, unit), unit)]
+
+    def out_local(v):
+        slot = lax.rem(v, 2)
+        return pltpu.make_async_copy(ob.at[slot], out_rows(v, c), o_local.at[slot])
+
+    def out_mate(v):
+        slot = lax.rem(v, 2)
+        return remote(ob.at[slot], out_rows(v, c), o_send.at[slot], o_recv.at[v // per], t, mate)
+
+    def merge_unit(v):
+        k, q = v // per, lax.rem(v, per)
+        slot = lax.rem(v, 2)
+        lanes = pl.ds(pl.multiple_of(q * unit, unit), unit)
+        second_hand(v)
+        factor = right[k, :, lanes]
+        squares = jnp.zeros((unit, 128), jnp.float32)
+        for n in range(tensor_count):
+            piece = g[v, n].astype(jnp.float32) + lax.dot_general(
+                factor, left[n, k], (((0,), (0,)), ((), ())), preferred_element_type=jnp.float32
+            )
+            merged[:, n * rows : (n + 1) * rows] = piece
+            for b in range(rows // 128):
+                part = piece[:, b * 128 : (b + 1) * 128]
+                squares = squares + part * part
+        total = jnp.sum(squares, axis=1, keepdims=True)
+        stack = lax.broadcasted_iota(jnp.int32, (stacks, unit), 0)
+        chosen = jnp.sum(jnp.where(stack == k, strength[:, lanes], 0.0), axis=0, keepdims=True)
+        wide = jnp.broadcast_to(chosen, (unit, unit)).T
+        scaling = wide / jnp.sqrt(total + 1e-06)
+
+        @pl.when(v >= 2)
+        def _():
+            out_local(v - 2).wait()
+            out_mate(v - 2).wait_send()
+
+        for b in range(tensor_count * rows // 128):
+            at = slice(b * 128, (b + 1) * 128)
+            ob[slot, :, at] = (merged[:, at] * scaling).astype(ob.dtype)
+        out_local(v).start()
+        out_mate(v).start()
+
+    carrier = lax.rem(t, 2) == c
+
+    def left_out(ts):
+        return remote(lt, left.at[t], l_send.at[ts], l_recv.at[t], ts, d)
+
+    def left_mate(ts):
+        return remote(left.at[ts], left.at[ts], l_mate.at[ts], l_recv.at[ts], t, mate)
+
+    def left_twin(ts):
+        return remote(left.at[ts], left.at[ts], l_twin.at[ts], l_recv.at[ts], t, twin)
+
+    own_left = pltpu.make_async_copy(lt, left.at[t], l_own)
+
+    def factors(h, dp):
+        at = pl.multiple_of(lax.rem(t, group) * serve + h * half, unit)
+        way = dp // 2
+        return (
+            remote(r.at[:, :, pl.ds(at, half)], right, p_send.at[0, way, h], p_recv.at[0], t, dp),
+            remote(m.at[:, pl.ds(at, half)], strength, p_send.at[1, way, h], p_recv.at[1], t, dp),
+        )
+
+    def own_factors(h):
+        at = pl.multiple_of(lax.rem(t, group) * serve + h * half, unit)
+        return (
+            pltpu.make_async_copy(r.at[:, :, pl.ds(at, half)], right, p_recv.at[0]),
+            pltpu.make_async_copy(m.at[:, pl.ds(at, half)], strength, p_recv.at[1]),
+        )
+
+    def each_factor(remote_do, own_do):
+        for way in range(2):
+            for h in range(2):
+                dp = way * 2 + h
+
+                if remote_do:
+
+                    @pl.when(jnp.logical_and(home, d != dp))
+                    def _():
+                        for copy in factors(h, dp):
+                            remote_do(copy)
+
+                if own_do:
+
+                    @pl.when(jnp.logical_and(home, d == dp))
+                    def _():
+                        for copy in own_factors(h):
+                            own_do(copy)
+
+    start_load(0)
+    start_load(1)
+    own_left.start()
+    flip_and_send(0)
+
+    @pl.when(carrier)
+    def _():
+        loop(half_t, lambda i: left_out(near_source(i)).start(), 1)
+
+        @pl.when(far)
+        def _():
+            loop(half_t, lambda i: left_out(far_source(i)).start())
+
+    each_factor(lambda copy: copy.start(), lambda copy: copy.start())
+    loop(AHEAD, flip_and_send, 1)
+    loop(RELAY_AHEAD, relay_step)
+
+    def spread_left(ts, across):
+        left_mate(ts).wait_recv()
+
+        @pl.when(lax.rem(ts, 2) == c)
+        def _():
+            left_mate(ts).start()
+            if across:
+
+                @pl.when(near)
+                def _():
+                    left_twin(ts).start()
+
+    loop(half_t, lambda i: spread_left(near_source(i), False), 1)
+    loop(half_t, lambda i: spread_left(far_source(i), True))
+    own_left.wait()
+
+    @pl.when(jnp.logical_not(home))
+    def _():
+        for copy in factors(0, mate):
+            copy.wait_recv()
+
+    each_factor(None, lambda copy: copy.wait())
+
+    def step(v):
+        @pl.when(v + AHEAD < units)
+        def _():
+            flip_and_send(v + AHEAD)
+
+        @pl.when(v + RELAY_AHEAD < units)
+        def _():
+            relay_step(v + RELAY_AHEAD)
+
+        arrivals(v)
+
+        @pl.when(v >= MERGE_LAG)
+        def _():
+            merge_unit(v - MERGE_LAG)
+
+    loop(units, step)
+    loop(units, merge_unit, units - MERGE_LAG)
+
+    for v in (units - 2, units - 1):
+        out_local(v).wait()
+        out_mate(v).wait_send()
+    for k in range(stacks):
+        rows_in = o.at[k, pl.ds(pl.multiple_of((1 - c) * half, unit), half)]
+        remote(rows_in, rows_in, o_send.at[0], o_recv.at[k], t, mate).wait_recv()
+    for k in range(stacks):
+        for j, h in pairs:
+
+            @pl.when(jnp.logical_not(stays(j, h)))
+            def _():
+                sent = s.at[k * per : (k + 1) * per, j, h]
+                remote(sent, sent, s_send.at[k, j, h], g_recv.at[0, 0], t, twin).wait_send()
+
+    @pl.when(near)
+    def _():
+        for j, h in pairs:
+            sent = rb.at[0 : units - (units + 1 + h) // 3, j, h]
+            remote(sent, sent, rb_send.at[j, h], g_recv.at[0, 0], t, twin).wait_send()
+
+    def sent_on(ts, count):
+        sent = g.at[0:count, ts]
+        remote(sent, sent, f_send.at[ts], g_recv.at[0, 0], t, twin).wait_send()
+
+    @pl.when(near)
+    def _():
+        loop(half_t, lambda i: sent_on(near_source(i), units))
+
+    for h in range(2):
+        count = (units + 1 + h) // 3
+
+        @pl.when(jnp.logical_and(near, c == h))
+        def _():
+            loop(half_t, lambda i: sent_on(far_source(i), count))
+
+        @pl.when(jnp.logical_and(far, c == h))
+        def _():
+            loop(half_t, lambda i: sent_on(far_source(i), units - count))
+
+    @pl.when(carrier)
+    def _():
+        loop(half_t, lambda i: left_out(near_source(i)).wait_send(), 1)
+
+        @pl.when(far)
+        def _():
+            loop(half_t, lambda i: left_out(far_source(i)).wait_send())
+
+    def left_sent(ts, across):
+        @pl.when(lax.rem(ts, 2) == c)
+        def _():
+            left_mate(ts).wait_send()
+            if across:
+
+                @pl.when(near)
+                def _():
+                    left_twin(ts).wait_send()
+
+    loop(half_t, lambda i: left_sent(near_source(i), False), 1)
+    loop(half_t, lambda i: left_sent(far_source(i), True))
+    each_factor(lambda copy: copy.wait_send(), None)
+
+
+def fused(w, lt, r, m, tensor_count):
+    stacks, rows, cols = w.shape
+    rank = lt.shape[1]
+    group = tensor_count // 4
+    serve = cols // group
+    half = serve // 2
+    per = half // UNIT
+    units = stacks * per
+    relayed = units - (units + 1) // 3
+    dma = pltpu.SemaphoreType.DMA
+    hbm = pl.BlockSpec(memory_space=pl.ANY)
+    width = tensor_count * rows
+    return pl.pallas_call(
+        functools.partial(fused_kernel, tensor_count),
+        out_shape=jax.ShapeDtypeStruct((stacks, serve, width), w.dtype),
+        in_specs=[hbm] * 4,
+        out_specs=hbm,
+        scratch_shapes=[
+            pltpu.VMEM((units, group, 2, UNIT, rows), w.dtype),
+            pltpu.VMEM((units, tensor_count, UNIT, rows), w.dtype),
+            pltpu.VMEM((relayed, group, 2, UNIT, rows), w.dtype),
+            pltpu.VMEM((2, group, 2, rows, UNIT), w.dtype),
+            pltpu.VMEM((tensor_count, stacks, rank, rows), w.dtype),
+            pltpu.VMEM((stacks, rank, half), w.dtype),
+            pltpu.VMEM((stacks, half), jnp.float32),
+            pltpu.VMEM((UNIT, width), jnp.float32),
+            pltpu.VMEM((2, UNIT, width), w.dtype),
+            dma((2, group, 2)),
+            dma((stacks, group, 2)),
+            dma((units, tensor_count)),
+            dma((relayed, group, 2)),
+            dma((group, 2)),
+            dma((tensor_count,)),
+            dma,
+            dma((tensor_count,)),
+            dma((tensor_count,)),
+            dma((tensor_count,)),
+            dma((tensor_count,)),
+            dma((2,)),
+            dma((2, 2, 2)),
+            dma((2,)),
+            dma((2,)),
+            dma((stacks,)),
+        ],
+        compiler_params=pltpu.CompilerParams(has_side_effects=True, vmem_limit_bytes=67_043_328),
+    )(w, lt, r, m)
+
+
+def fits(tensor_count, replica_count, stacks, rows, cols):
+    if replica_count != 4 or tensor_count % 4 or cols % (tensor_count // 4):
+        return False
+    serve = cols // (tensor_count // 4)
+    pieces = 7 * stacks * rows * cols // 6 + stacks * (serve // 2) * tensor_count * rows
+    return rows % 128 == 0 and serve % (2 * UNIT) == 0 and pieces <= 30_000_000
+
+
 def shards(base_weight, adapter_left, adapter_right, magnitude):
     tensor_count = lax.axis_size("tensor")
     replica_count = lax.axis_size("dp")
@@ -312,6 +742,15 @@
     chunks = stacks if tensor_count <= 16 else 1
     relayed = (2 * (serve // 16) + 1) // 3 * 16
 
+    if fits(tensor_count, replica_count, stacks, rows, cols):
+        out = fused(
+            base_weight.reshape(stacks, rows, cols),
+            adapter_left.swapaxes(2, 3).reshape(stacks, rank, rows),
+            adapter_right.reshape(stacks, rank, cols),
+            magnitude.reshape(stacks, cols).astype(jnp.float32),
+            tensor_count,
+        )
+        return out.reshape(experts, projections, serve, -1)
     s = flip(base_weight.reshape(stacks, rows, cols))
     if chunks == 1:
         s = s.reshape(1, stacks, group, serve, rows).swapaxes(1, 2)

time: 662 us -> 515 us (0.78)
  Pallas kernels: 576 us -> 467 us
  blocking collectives: 63 us -> 0 us
  local copies, waits for them, and re-layouts: 7.72 us -> 40.6 us
  between operations: 13.4 us -> 0.01 us
    pallas_call x3 -> x1, Pallas kernels: 576 us -> 467 us  [fused(): pl.pallas_call(functools.partial(fused_kernel, tensor_count), out_shape=j...]
    all_gather x2 -> x0, blocking collectives: 63 us -> none  [the longest x1 56.4 us: shards(): lax.all_gather(adapter_left.swapaxes(2, 3), 'tensor', axis=3, tiled=True)]
    unnamed x2 -> x1, local copies, waits for them, and re-layouts: 0.01 us -> 39.2 us
  transfers between devices with their start and end apart: 1 -> 0, of which waited for: 0 -> 0; matrix products, arithmetic and copies ran while one was open for 1% -> 0% of each run, Pallas kernels for 78% -> 0%
where the time goes in v1:
time: 515 us; the launch traced here: 508 us
  Pallas kernels  467 us (91%)
  local copies, waits for them, and re-layouts  40.6 us (8%)
    pallas_call x1, Pallas kernels, fused(): pl.pallas_call(functools.partial(fused_kernel, tensor_count), out_shape=j...  467 us
    unnamed x1, local copies, waits for them, and re-layouts  39.2 us

profile of v1, /device:TPU:0, one launch (start us, length us, event | category | flops | bytes accessed | tf_op | source)
XLA Modules:
  0.0 507.5 jit_solution(16159955493566852904)
XLA Ops:
  0.0 1.4 reshape.19.m
  1.4 467.0 %shard_map.46 = bf16[4,1792,4096]{2,1,0:T(8,128)(2,1)} custom-call(bf16[4,512,3584]{2,1,0:T(8,128)(2,1)} %bitcast.7, bf16[4,16,512]{2,1,0:T(8,128)(2,1)} %bitcast.9, bf16[4,16,3584]{2,1,0:T(8,128)(2,1)} %bitcast.8, f32[4,3584]{1,0:T(4,128)} %reshape.19.m), custom_call_target="tpu_custom_call" | custom-call | tf_op jit(solution)/shard_map/pallas_call | solution.py:690
  468.4 39.2 %copy.6 = bf16[2,2,1792,4096]{3,2,1,0:T(8,128)(2,1)} copy(bf16[2,2,1792,4096]{3,2,1,0:T(8,128)(2,1)} %bitcast.6) | data formatting | bytes 117440512

commit v2 on v1

--- a/solution.py
+++ b/solution.py
@@ -302,21 +302,21 @@
 
 
 UNIT = 128
-AHEAD, RELAY_AHEAD, MERGE_LAG = 4, 2, 1
+RELAY_LAG, FORWARD_LAG, MERGE_LAG = 1, 2, 2
+CREDIT_LAG, KEPT = 3, 8
 
 
 def fused_kernel(
-    tensor_count, w, lt, r, m, o, s, g, rb, win, left, right, strength, merged, ob,
-    w_sem, s_send, g_recv, rb_recv, rb_send, f_send, l_own, l_recv, l_send, l_mate, l_twin,
-    p_recv, p_send, o_local, o_send, o_recv,
+    tensor_count, lead, w, lt, r, m, first, middle, s, g, rb, win, left, right, strength, merged,
+    w_sem, s_send, s_twin, g_recv, rb_recv, rb_send, f_send, l_own, l_recv, l_send, l_mate, l_twin,
+    p_recv, p_send, o_send, o_recv, credit,
 ):
     units, _, unit, rows = g.shape
-    group = s.shape[1]
     half_t = tensor_count // 2
-    serve = o.shape[1]
-    half = serve // 2
+    group = half_t // 2
+    stacks, half = strength.shape
+    serve = 2 * half
     per = half // unit
-    stacks = units // per
     t, d = lax.axis_index("tensor"), lax.axis_index("dp")
     x, c = d // 2, lax.rem(d, 2)
     twin = lax.rem(d + 2, 4)
@@ -365,16 +365,27 @@
         for j, h in pairs:
             load(v, j, h).start()
 
+    def piece(v, j, h):
+        return s.at[v // 2, lax.rem(v, 2) * half_t + j * 2 + h]
+
     def to_server(v, j, h):
         return remote(
-            s.at[v, j, h], g.at[v, t], s_send.at[v // per, j, h], g_recv.at[v, t],
+            piece(v, j, h), g.at[v, t], s_send.at[v // 2, j, h], g_recv.at[v, t],
             d * group + j, x * 2 + h,
+        )
+
+    level = jnp.logical_and(near, d == t // group)
+
+    def to_twin_server(v, j, h):
+        return remote(
+            piece(v, j, h), g.at[v, t], s_twin.at[v // 2, j, h], g_recv.at[v, t],
+            d * group + j, (1 - x) * 2 + h,
         )
 
     def to_relay(v, j, h):
         at = relay_index(v, h)
         return remote(
-            s.at[v, j, h], rb.at[at, j, h], s_send.at[v // per, j, h], rb_recv.at[at, j, h], t, twin
+            piece(v, j, h), rb.at[at, j, h], s_send.at[v // 2, j, h], rb_recv.at[at, j, h], t, twin
         )
 
     def stays(j, h):
@@ -385,7 +396,7 @@
         for j, h in pairs:
             load(v, j, h).wait()
             turned = win[slot, j, h].T
-            s[v, j, h] = turned
+            s[v // 2, lax.rem(v, 2) * half_t + j * 2 + h] = turned
             own = stays(j, h)
 
             @pl.when(own)
@@ -401,6 +412,10 @@
             @pl.when(jnp.logical_not(jnp.logical_or(own, by_hand)))
             def _():
                 to_server(v, j, h).start()
+
+            @pl.when(level)
+            def _():
+                to_twin_server(v, j, h).start()
 
         @pl.when(v + 2 < units)
         def _():
@@ -421,7 +436,7 @@
                 relay(v, j, h).start()
 
     def forward(v, ts):
-        return remote(g.at[v, ts], g.at[v, ts], f_send.at[ts], g_recv.at[v, ts], t, twin)
+        return remote(g.at[v, ts], g.at[v, ts], f_send.at[v, ts], g_recv.at[v, ts], t, twin)
 
     def got(v, ts):
         forward(v, ts).wait_recv()
@@ -433,15 +448,19 @@
     def arrivals(v):
         @pl.when(near)
         def _():
-            @pl.when(home)
-            def _():
-                forward(v, t).start()
-
             @pl.when(jnp.logical_not(home))
             def _():
-                pass_on(v, t)
-
-            loop(half_t, lambda i: pass_on(v, near_source(i)), 1)
+                got(v, t)
+
+            def take_near(i):
+                ts = near_source(i)
+                got(v, ts)
+
+                @pl.when(ts // group != t // group)
+                def _():
+                    forward(v, ts).start()
+
+            loop(half_t, take_near, 1)
 
             @pl.when(is_direct(v, c))
             def _():
@@ -464,21 +483,58 @@
         def _():
             loop(half_t, lambda i: got(v, far_source(i)))
 
-    def out_rows(v, core):
-        k, q = v // per, lax.rem(v, per)
-        return o.at[k, pl.ds(pl.multiple_of(core * half + q * unit, unit), unit)]
-
-    def out_local(v):
-        slot = lax.rem(v, 2)
-        return pltpu.make_async_copy(ob.at[slot], out_rows(v, c), o_local.at[slot])
-
-    def out_mate(v):
-        slot = lax.rem(v, 2)
-        return remote(ob.at[slot], out_rows(v, c), o_send.at[slot], o_recv.at[v // per], t, mate)
+    def forwarded(v):
+        def near_sent(i):
+            @pl.when(near_source(i) // group != t // group)
+            def _():
+                forward(v, near_source(i)).wait_send()
+
+        @pl.when(near)
+        def _():
+            loop(half_t, near_sent)
+
+        @pl.when(near == is_direct(v, c))
+        def _():
+            loop(half_t, lambda i: forward(v, far_source(i)).wait_send())
+
+    def to_mate(v, place):
+        return remote(g.at[v], place, o_send.at[v], o_recv.at[v], t, mate)
+
+    spare = units // 2
+
+    def hand_to_mate(v):
+        @pl.when(v < lead)
+        def _():
+            to_mate(v, first.at[v]).start()
+
+        @pl.when(jnp.logical_and(v >= lead, v < spare))
+        def _():
+            to_mate(v, middle.at[v - lead]).start()
+
+        @pl.when(v >= spare)
+        def _():
+            pl.semaphore_wait(credit, 1)
+            to_mate(v, s.at[v - spare]).start()
+
+    def give_credit(v):
+        at = v - spare
+        both = s.at[at, 0:2]
+        for j, h in pairs:
+
+            @pl.when(jnp.logical_not(stays(j, h)))
+            def _():
+                remote(both, both, s_send.at[at, j, h], o_recv.at[0], t, mate).wait_send()
+
+            @pl.when(level)
+            def _():
+                remote(both, both, s_twin.at[at, j, h], o_recv.at[0], t, mate).wait_send()
+
+        pl.semaphore_signal(
+            credit, inc=1, device_id={"tensor": t, "dp": mate}, device_id_type=MESH
+        )
 
     def merge_unit(v):
         k, q = v // per, lax.rem(v, per)
-        slot = lax.rem(v, 2)
         lanes = pl.ds(pl.multiple_of(q * unit, unit), unit)
         second_hand(v)
         factor = right[k, :, lanes]
@@ -497,16 +553,13 @@
         wide = jnp.broadcast_to(chosen, (unit, unit)).T
         scaling = wide / jnp.sqrt(total + 1e-06)
 
-        @pl.when(v >= 2)
-        def _():
-            out_local(v - 2).wait()
-            out_mate(v - 2).wait_send()
-
-        for b in range(tensor_count * rows // 128):
-            at = slice(b * 128, (b + 1) * 128)
-            ob[slot, :, at] = (merged[:, at] * scaling).astype(ob.dtype)
-        out_local(v).start()
-        out_mate(v).start()
+        forwarded(v)
+        for n in range(tensor_count):
+            for b in range(rows // 128):
+                at = slice(b * 128, (b + 1) * 128)
+                wide_at = slice(n * rows + b * 128, n * rows + (b + 1) * 128)
+                g[v, n, :, at] = (merged[:, wide_at] * scaling).astype(g.dtype)
+        hand_to_mate(v)
 
     carrier = lax.rem(t, 2) == c
 
@@ -558,7 +611,6 @@
     start_load(0)
     start_load(1)
     own_left.start()
-    flip_and_send(0)
 
     @pl.when(carrier)
     def _():
@@ -569,63 +621,86 @@
             loop(half_t, lambda i: left_out(far_source(i)).start())
 
     each_factor(lambda copy: copy.start(), lambda copy: copy.start())
-    loop(AHEAD, flip_and_send, 1)
-    loop(RELAY_AHEAD, relay_step)
-
-    def spread_left(ts, across):
-        left_mate(ts).wait_recv()
-
-        @pl.when(lax.rem(ts, 2) == c)
-        def _():
+
+    def carries(ts):
+        return lax.rem(ts, 2) == c
+
+    def spread(ts, across):
+        @pl.when(carries(ts))
+        def _():
+            left_mate(ts).wait_recv()
             left_mate(ts).start()
             if across:
-
-                @pl.when(near)
-                def _():
-                    left_twin(ts).start()
-
-    loop(half_t, lambda i: spread_left(near_source(i), False), 1)
-    loop(half_t, lambda i: spread_left(far_source(i), True))
-    own_left.wait()
-
-    @pl.when(jnp.logical_not(home))
-    def _():
-        for copy in factors(0, mate):
-            copy.wait_recv()
-
-    each_factor(None, lambda copy: copy.wait())
-
-    def step(v):
-        @pl.when(v + AHEAD < units)
-        def _():
-            flip_and_send(v + AHEAD)
-
-        @pl.when(v + RELAY_AHEAD < units)
-        def _():
-            relay_step(v + RELAY_AHEAD)
-
-        arrivals(v)
-
-        @pl.when(v >= MERGE_LAG)
-        def _():
-            merge_unit(v - MERGE_LAG)
-
-    loop(units, step)
-    loop(units, merge_unit, units - MERGE_LAG)
-
-    for v in (units - 2, units - 1):
-        out_local(v).wait()
-        out_mate(v).wait_send()
-    for k in range(stacks):
-        rows_in = o.at[k, pl.ds(pl.multiple_of((1 - c) * half, unit), half)]
-        remote(rows_in, rows_in, o_send.at[0], o_recv.at[k], t, mate).wait_recv()
-    for k in range(stacks):
-        for j, h in pairs:
-
-            @pl.when(jnp.logical_not(stays(j, h)))
-            def _():
-                sent = s.at[k * per : (k + 1) * per, j, h]
-                remote(sent, sent, s_send.at[k, j, h], g_recv.at[0, 0], t, twin).wait_send()
+                left_twin(ts).start()
+
+    def take(ts):
+        @pl.when(jnp.logical_not(carries(ts)))
+        def _():
+            left_mate(ts).wait_recv()
+
+    def spread_first():
+        loop(half_t, lambda i: spread(near_source(i), False), 1)
+
+        @pl.when(near)
+        def _():
+            loop(half_t, lambda i: spread(far_source(i), True))
+
+    def spread_second():
+        @pl.when(far)
+        def _():
+            loop(half_t, lambda i: spread(far_source(i), False))
+
+    def take_factors():
+        own_left.wait()
+        loop(half_t, lambda i: take(near_source(i)), 1)
+        loop(half_t, lambda i: take(far_source(i)))
+
+        @pl.when(jnp.logical_not(home))
+        def _():
+            for copy in factors(0, mate):
+                copy.wait_recv()
+
+        each_factor(None, lambda copy: copy.wait())
+
+    def step(u):
+        @pl.when(u < units)
+        def _():
+            flip_and_send(u)
+
+        v = u - RELAY_LAG
+
+        @pl.when(jnp.logical_and(v >= 0, v < units))
+        def _():
+            relay_step(v)
+
+        v = u - FORWARD_LAG
+
+        @pl.when(jnp.logical_and(v >= 0, v < units))
+        def _():
+            arrivals(v)
+
+        v = u - CREDIT_LAG
+
+        @pl.when(jnp.logical_and(v >= spare, v < units))
+        def _():
+            give_credit(v)
+
+        for at, what in enumerate((spread_first, spread_second, take_factors)):
+            pl.when(u == FORWARD_LAG + at)(what)
+
+        v = u - FORWARD_LAG - MERGE_LAG
+
+        @pl.when(v >= 0)
+        def _():
+            merge_unit(v)
+
+    loop(units + FORWARD_LAG + MERGE_LAG, step)
+
+    def last(v):
+        to_mate(v, g.at[v]).wait_send()
+        to_mate(v, g.at[v]).wait_recv()
+
+    loop(units, last)
 
     @pl.when(near)
     def _():
@@ -633,25 +708,6 @@
             sent = rb.at[0 : units - (units + 1 + h) // 3, j, h]
             remote(sent, sent, rb_send.at[j, h], g_recv.at[0, 0], t, twin).wait_send()
 
-    def sent_on(ts, count):
-        sent = g.at[0:count, ts]
-        remote(sent, sent, f_send.at[ts], g_recv.at[0, 0], t, twin).wait_send()
-
-    @pl.when(near)
-    def _():
-        loop(half_t, lambda i: sent_on(near_source(i), units))
-
-    for h in range(2):
-        count = (units + 1 + h) // 3
-
-        @pl.when(jnp.logical_and(near, c == h))
-        def _():
-            loop(half_t, lambda i: sent_on(far_source(i), count))
-
-        @pl.when(jnp.logical_and(far, c == h))
-        def _():
-            loop(half_t, lambda i: sent_on(far_source(i), units - count))
-
     @pl.when(carrier)
     def _():
         loop(half_t, lambda i: left_out(near_source(i)).wait_send(), 1)
@@ -673,6 +729,55 @@
     loop(half_t, lambda i: left_sent(near_source(i), False), 1)
     loop(half_t, lambda i: left_sent(far_source(i), True))
     each_factor(lambda copy: copy.wait_send(), None)
+
+
+def place_kernel(stacks, first, middle, last, own, o, held, stage, in_sem, out_sem):
+    c = lax.rem(lax.axis_index("dp"), 2)
+    units, count, unit, rows = own.shape
+    half = o.shape[1] // 2
+    per = units // stacks
+    lead, kept = first.shape[0], middle.shape[0]
+    depth = stage.shape[0]
+
+    def fetch(v):
+        slot = lax.rem(v, 2)
+        return pltpu.make_async_copy(first.at[v], held.at[slot], in_sem.at[slot])
+
+    def leave(slot, k, at):
+        return pltpu.make_async_copy(stage.at[slot], o.at[k, at], out_sem.at[slot])
+
+    def place(src, v, core, turn):
+        k, q = v // per, lax.rem(v, per)
+        at = pl.ds(pl.multiple_of(core * half + q * unit, unit), unit)
+        slot = lax.rem(turn, depth)
+
+        @pl.when(turn >= depth)
+        def _():
+            leave(slot, k, at).wait()
+
+        for n in range(count):
+            stage[slot, :, n * rows : (n + 1) * rows] = src[n]
+        leave(slot, k, at).start()
+
+    def loop(begin, end, body):
+        lax.fori_loop(begin, end, lambda v, carry: (body(v), carry)[1], 0)
+
+    def from_hbm(v):
+        fetch(v).wait()
+        place(held.at[lax.rem(v, 2)], v, 1 - c, units + v)
+
+        @pl.when(v + 2 < lead)
+        def _():
+            fetch(v + 2).start()
+
+    for v in range(min(2, lead)):
+        fetch(v).start()
+    loop(0, units, lambda v: place(own.at[v], v, c, v))
+    loop(0, lead, from_hbm)
+    loop(lead, lead + kept, lambda v: place(middle.at[v - lead], v, 1 - c, units + v))
+    loop(lead + kept, units, lambda v: place(last.at[v - lead - kept], v, 1 - c, units + v))
+    for slot in range(depth):
+        leave(slot, 0, pl.ds(0, unit)).wait()
 
 
 def fused(w, lt, r, m, tensor_count):
@@ -687,27 +792,34 @@
     dma = pltpu.SemaphoreType.DMA
     hbm = pl.BlockSpec(memory_space=pl.ANY)
     width = tensor_count * rows
-    return pl.pallas_call(
-        functools.partial(fused_kernel, tensor_count),
-        out_shape=jax.ShapeDtypeStruct((stacks, serve, width), w.dtype),
+    vmem = pl.BlockSpec(memory_space=pltpu.VMEM)
+    spare = units // 2
+    lead = max(1, spare - KEPT)
+    block = (tensor_count, UNIT, rows)
+    parts = pl.pallas_call(
+        functools.partial(fused_kernel, tensor_count, lead),
+        out_shape=(
+            jax.ShapeDtypeStruct((lead, *block), w.dtype),
+            pltpu.VMEM((spare - lead, *block), w.dtype),
+            pltpu.VMEM((spare, *block), w.dtype),
+            pltpu.VMEM((units, *block), w.dtype),
+        ),
         in_specs=[hbm] * 4,
-        out_specs=hbm,
+        out_specs=(hbm, vmem, vmem, vmem),
         scratch_shapes=[
-            pltpu.VMEM((units, group, 2, UNIT, rows), w.dtype),
-            pltpu.VMEM((units, tensor_count, UNIT, rows), w.dtype),
             pltpu.VMEM((relayed, group, 2, UNIT, rows), w.dtype),
             pltpu.VMEM((2, group, 2, rows, UNIT), w.dtype),
             pltpu.VMEM((tensor_count, stacks, rank, rows), w.dtype),
             pltpu.VMEM((stacks, rank, half), w.dtype),
             pltpu.VMEM((stacks, half), jnp.float32),
             pltpu.VMEM((UNIT, width), jnp.float32),
-            pltpu.VMEM((2, UNIT, width), w.dtype),
             dma((2, group, 2)),
-            dma((stacks, group, 2)),
+            dma((spare, group, 2)),
+            dma((spare, group, 2)),
             dma((units, tensor_count)),
             dma((relayed, group, 2)),
             dma((group, 2)),
-            dma((tensor_count,)),
+            dma((units, tensor_count)),
             dma,
             dma((tensor_count,)),
             dma((tensor_count,)),
@@ -715,20 +827,33 @@
             dma((tensor_count,)),
             dma((2,)),
             dma((2, 2, 2)),
+            dma((units,)),
+            dma((units,)),
+            pltpu.SemaphoreType.REGULAR,
+        ],
+        compiler_params=pltpu.CompilerParams(has_side_effects=True, vmem_limit_bytes=14200000),
+    )(w, lt, r, m)
+    return pl.pallas_call(
+        functools.partial(place_kernel, stacks),
+        out_shape=jax.ShapeDtypeStruct((stacks, serve, width), w.dtype),
+        in_specs=[hbm, vmem, vmem, vmem],
+        out_specs=hbm,
+        scratch_shapes=[
+            pltpu.VMEM((2, *block), w.dtype),
+            pltpu.VMEM((4, UNIT, width), w.dtype),
             dma((2,)),
-            dma((2,)),
-            dma((stacks,)),
+            dma((4,)),
         ],
-        compiler_params=pltpu.CompilerParams(has_side_effects=True, vmem_limit_bytes=67_043_328),
-    )(w, lt, r, m)
+        compiler_params=pltpu.CompilerParams(vmem_limit_bytes=8_000_000),
+    )(parts[0], *(pltpu.with_memory_space_constraint(p, pltpu.VMEM) for p in parts[1:]))
 
 
 def fits(tensor_count, replica_count, stacks, rows, cols):
-    if replica_count != 4 or tensor_count % 4 or cols % (tensor_count // 4):
+    if replica_count != 4 or tensor_count % 8 or cols % (tensor_count // 2 * UNIT) or rows % 128:
         return False
-    serve = cols // (tensor_count // 4)
-    pieces = 7 * stacks * rows * cols // 6 + stacks * (serve // 2) * tensor_count * rows
-    return rows % 128 == 0 and serve % (2 * UNIT) == 0 and pieces <= 30_000_000
+    units = stacks * (cols // (tensor_count // 2 * UNIT))
+    pieces = units * tensor_count * UNIT * rows
+    return units % 2 == 0 and units // 2 > KEPT and pieces <= 15_000_000
 
 
 def shards(base_weight, adapter_left, adapter_right, magnitude):

time: 515 us -> 477 us (0.926)
  local copies, waits for them, and re-layouts: 40.6 us -> 1.39 us
    unnamed x1 -> x0, local copies, waits for them, and re-layouts: 39.2 us -> none
    pallas_call x1 -> x2, Pallas kernels: 467 us -> 471 us  [the longest x1 449 us: fused(): pl.pallas_call(functools.partial(fused_kernel, tensor_count, lead), out_s...]
where the time goes in v2:
time: 477 us; the launch traced here: 472 us
  Pallas kernels  471 us (99%)
    pallas_call x1, Pallas kernels, fused(): pl.pallas_call(functools.partial(fused_kernel, tensor_count, lead), out_s...  449 us
    pallas_call x1, Pallas kernels, fused(): pl.pallas_call(functools.partial(place_kernel, stacks), out_shape=jax.Sha...  21.7 us

profile of v2, /device:TPU:0, one launch (start us, length us, event | category | flops | bytes accessed | tf_op | source)
XLA Modules:
  0.0 472.2 jit_solution(5050658822484639953)
XLA Ops:
  0.0 1.4 reshape.19.m
  1.4 449.1 %shard_map.46 = (bf16[6,8,128,512]{3,2,1,0:T(8,128)(2,1)}, bf16[8,8,128,512]{3,2,1,0:T(8,128)(2,1)S(1)}, bf16[14,8,128,512]{3,2,1,0:T(8,128)(2,1)S(1)}, bf16[28,8,128,512]{3,2,1,0:T(8,128)(2,1)S(1)}) custom-call(bf16[4,512,3584]{2,1,0:T(8,128)(2,1)} %bitcast.6, bf16[4,16,512]{2,1,0:T(8,128)(2,1)} %bitcast.8, bf16[4,16,3584]{2,1,0:T(8,128)(2,1)} %bitcast.7, ...), custom_call_target="tpu_custom_call" | custom-call | tf_op jit(solution)/shard_map/pallas_call | solution.py:799
  450.5 21.7 %shard_map.47 = bf16[4,1792,4096]{2,1,0:T(8,128)(2,1)} custom-call(bf16[6,8,128,512]{3,2,1,0:T(8,128)(2,1)} %get-tuple-element.9.first, bf16[8,8,128,512]{3,2,1,0:T(8,128)(2,1)S(1)} %get-tuple-element.10.middle, bf16[14,8,128,512]{3,2,1,0:T(8,128)(2,1)S(1)} %get-tuple-element.11.last, bf16[28,8,128,512]{3,2,1,0:T(8,128)(2,1)S(1)} %get-tuple-element.12.own), custom_call_target="tpu_custom_call" | custom-call | tf_op jit(solution)/shard_map/pallas_call | solution.py:836

commit v3 on v2

--- a/solution.py
+++ b/solution.py
@@ -303,7 +303,7 @@
 
 UNIT = 128
 RELAY_LAG, FORWARD_LAG, MERGE_LAG = 1, 2, 2
-CREDIT_LAG, KEPT = 3, 8
+CREDIT_LAG, KEPT, STAGED = 3, 8, 6
 
 
 def fused_kernel(
@@ -314,7 +314,7 @@
     units, _, unit, rows = g.shape
     half_t = tensor_count // 2
     group = half_t // 2
-    stacks, half = strength.shape
+    experts, projections, half = strength.shape
     serve = 2 * half
     per = half // unit
     t, d = lax.axis_index("tensor"), lax.axis_index("dp")
@@ -548,8 +548,12 @@
                 part = piece[:, b * 128 : (b + 1) * 128]
                 squares = squares + part * part
         total = jnp.sum(squares, axis=1, keepdims=True)
-        stack = lax.broadcasted_iota(jnp.int32, (stacks, unit), 0)
-        chosen = jnp.sum(jnp.where(stack == k, strength[:, lanes], 0.0), axis=0, keepdims=True)
+        row = lax.broadcasted_iota(jnp.int32, (projections, unit), 0)
+        chosen = jnp.zeros((1, unit), jnp.float32)
+        for e in range(experts):
+            line = strength[e, :, lanes].astype(jnp.float32)
+            line = jnp.where(row + e * projections == k, line, 0.0)
+            chosen = chosen + jnp.sum(line, axis=0, keepdims=True)
         wide = jnp.broadcast_to(chosen, (unit, unit)).T
         scaling = wide / jnp.sqrt(total + 1e-06)
 
@@ -579,14 +583,14 @@
         way = dp // 2
         return (
             remote(r.at[:, :, pl.ds(at, half)], right, p_send.at[0, way, h], p_recv.at[0], t, dp),
-            remote(m.at[:, pl.ds(at, half)], strength, p_send.at[1, way, h], p_recv.at[1], t, dp),
+            remote(m.at[:, :, pl.ds(at, half)], strength, p_send.at[1, way, h], p_recv.at[1], t, dp),
         )
 
     def own_factors(h):
         at = pl.multiple_of(lax.rem(t, group) * serve + h * half, unit)
         return (
             pltpu.make_async_copy(r.at[:, :, pl.ds(at, half)], right, p_recv.at[0]),
-            pltpu.make_async_copy(m.at[:, pl.ds(at, half)], strength, p_recv.at[1]),
+            pltpu.make_async_copy(m.at[:, :, pl.ds(at, half)], strength, p_recv.at[1]),
         )
 
     def each_factor(remote_do, own_do):
@@ -611,6 +615,19 @@
     start_load(0)
     start_load(1)
     own_left.start()
+    barrier = pltpu.get_barrier_semaphore()
+
+    def greet(i):
+        to, at = i // 4, lax.rem(i, 4)
+
+        @pl.when(jnp.logical_or(to != t, at != d))
+        def _():
+            pl.semaphore_signal(
+                barrier, inc=1, device_id={"tensor": to, "dp": at}, device_id_type=MESH
+            )
+
+    loop(4 * tensor_count, greet)
+    pl.semaphore_wait(barrier, 4 * tensor_count - 1)
 
     @pl.when(carrier)
     def _():
@@ -622,33 +639,46 @@
 
     each_factor(lambda copy: copy.start(), lambda copy: copy.start())
 
+    def left_round(ts, target):
+        return remote(left.at[ts], left.at[ts], l_twin.at[target], l_recv.at[ts], target, d)
+
     def carries(ts):
         return lax.rem(ts, 2) == c
 
-    def spread(ts, across):
+    def spread(ts):
         @pl.when(carries(ts))
         def _():
             left_mate(ts).wait_recv()
             left_mate(ts).start()
-            if across:
-                left_twin(ts).start()
 
     def take(ts):
         @pl.when(jnp.logical_not(carries(ts)))
         def _():
             left_mate(ts).wait_recv()
 
+    opposite = far_source(0)
+
     def spread_first():
-        loop(half_t, lambda i: spread(near_source(i), False), 1)
+        loop(half_t, lambda i: spread(near_source(i)), 1)
 
         @pl.when(near)
         def _():
-            loop(half_t, lambda i: spread(far_source(i), True))
+            loop(half_t, lambda i: spread(far_source(i)))
+
+            @pl.when(carries(opposite))
+            def _():
+                left_twin(opposite).start()
 
     def spread_second():
         @pl.when(far)
         def _():
-            loop(half_t, lambda i: spread(far_source(i), False))
+            spread(opposite)
+
+            @pl.when(carries(opposite))
+            def _():
+                loop(half_t, lambda i: left_round(opposite, near_source(i)).start(), 1)
+
+            loop(half_t, lambda i: spread(far_source(i)), 1)
 
     def take_factors():
         own_left.wait()
@@ -716,18 +746,24 @@
         def _():
             loop(half_t, lambda i: left_out(far_source(i)).wait_send())
 
-    def left_sent(ts, across):
-        @pl.when(lax.rem(ts, 2) == c)
+    def left_sent(ts):
+        @pl.when(carries(ts))
         def _():
             left_mate(ts).wait_send()
-            if across:
-
-                @pl.when(near)
-                def _():
-                    left_twin(ts).wait_send()
-
-    loop(half_t, lambda i: left_sent(near_source(i), False), 1)
-    loop(half_t, lambda i: left_sent(far_source(i), True))
+
+    loop(half_t, lambda i: left_sent(near_source(i)), 1)
+    loop(half_t, lambda i: left_sent(far_source(i)))
+
+    @pl.when(carries(opposite))
+    def _():
+        @pl.when(near)
+        def _():
+            left_twin(opposite).wait_send()
+
+        @pl.when(far)
+        def _():
+            loop(half_t, lambda i: left_round(opposite, near_source(i)).wait_send(), 1)
+
     each_factor(lambda copy: copy.wait_send(), None)
 
 
@@ -740,8 +776,7 @@
     depth = stage.shape[0]
 
     def fetch(v):
-        slot = lax.rem(v, 2)
-        return pltpu.make_async_copy(first.at[v], held.at[slot], in_sem.at[slot])
+        return pltpu.make_async_copy(first.at[v], held.at[v], in_sem.at[v])
 
     def leave(slot, k, at):
         return pltpu.make_async_copy(stage.at[slot], o.at[k, at], out_sem.at[slot])
@@ -764,14 +799,9 @@
 
     def from_hbm(v):
         fetch(v).wait()
-        place(held.at[lax.rem(v, 2)], v, 1 - c, units + v)
-
-        @pl.when(v + 2 < lead)
-        def _():
-            fetch(v + 2).start()
-
-    for v in range(min(2, lead)):
-        fetch(v).start()
+        place(held.at[v], v, 1 - c, units + v)
+
+    loop(0, lead, lambda v: fetch(v).start())
     loop(0, units, lambda v: place(own.at[v], v, c, v))
     loop(0, lead, from_hbm)
     loop(lead, lead + kept, lambda v: place(middle.at[v - lead], v, 1 - c, units + v))
@@ -811,7 +841,7 @@
             pltpu.VMEM((2, group, 2, rows, UNIT), w.dtype),
             pltpu.VMEM((tensor_count, stacks, rank, rows), w.dtype),
             pltpu.VMEM((stacks, rank, half), w.dtype),
-            pltpu.VMEM((stacks, half), jnp.float32),
+            pltpu.VMEM((*m.shape[:2], half), m.dtype),
             pltpu.VMEM((UNIT, width), jnp.float32),
             dma((2, group, 2)),
             dma((spare, group, 2)),
@@ -831,7 +861,9 @@
             dma((units,)),
             pltpu.SemaphoreType.REGULAR,
         ],
-        compiler_params=pltpu.CompilerParams(has_side_effects=True, vmem_limit_bytes=14200000),
+        compiler_params=pltpu.CompilerParams(
+            collective_id=0, has_side_effects=True, vmem_limit_bytes=14_200_000
+        ),
     )(w, lt, r, m)
     return pl.pallas_call(
         functools.partial(place_kernel, stacks),
@@ -839,12 +871,12 @@
         in_specs=[hbm, vmem, vmem, vmem],
         out_specs=hbm,
         scratch_shapes=[
-            pltpu.VMEM((2, *block), w.dtype),
-            pltpu.VMEM((4, UNIT, width), w.dtype),
-            dma((2,)),
-            dma((4,)),
+            pltpu.VMEM((lead, *block), w.dtype),
+            pltpu.VMEM((STAGED, UNIT, width), w.dtype),
+            dma((lead,)),
+            dma((STAGED,)),
         ],
-        compiler_params=pltpu.CompilerParams(vmem_limit_bytes=8_000_000),
+        compiler_params=pltpu.CompilerParams(vmem_limit_bytes=13_500_000),
     )(parts[0], *(pltpu.with_memory_space_constraint(p, pltpu.VMEM) for p in parts[1:]))
 
 
@@ -872,7 +904,7 @@
             base_weight.reshape(stacks, rows, cols),
             adapter_left.swapaxes(2, 3).reshape(stacks, rank, rows),
             adapter_right.reshape(stacks, rank, cols),
-            magnitude.reshape(stacks, cols).astype(jnp.float32),
+            magnitude,
             tensor_count,
         )
         return out.reshape(experts, projections, serve, -1)

time: 477 us -> 473 us (level)
  Pallas kernels: 471 us -> 465 us
where the time goes in v3:
time: 473 us; the launch traced here: 465 us
  Pallas kernels  465 us (98%)
    pallas_call x1, Pallas kernels, fused(): pl.pallas_call(functools.partial(fused_kernel, tensor_count, lead), out_s...  445 us
    pallas_call x1, Pallas kernels, fused(): pl.pallas_call(functools.partial(place_kernel, stacks), out_shape=jax.Sha...  20.2 us

profile of v3, /device:TPU:0, one launch (start us, length us, event | category | flops | bytes accessed | tf_op | source)
XLA Modules:
  0.0 465.3 jit_solution(15506025638626405623)
XLA Ops:
  0.0 445.1 %shard_map.46 = (bf16[6,8,128,512]{3,2,1,0:T(8,128)(2,1)}, bf16[8,8,128,512]{3,2,1,0:T(8,128)(2,1)S(1)}, bf16[14,8,128,512]{3,2,1,0:T(8,128)(2,1)S(1)}, bf16[28,8,128,512]{3,2,1,0:T(8,128)(2,1)S(1)}) custom-call(bf16[4,512,3584]{2,1,0:T(8,128)(2,1)} %bitcast.6, bf16[4,16,512]{2,1,0:T(8,128)(2,1)} %bitcast.8, bf16[4,16,3584]{2,1,0:T(8,128)(2,1)} %bitcast.7, ...), custom_call_target="tpu_custom_call" | custom-call | tf_op jit(solution)/shard_map/pallas_call | solution.py:829
  445.1 20.2 %shard_map.47 = bf16[4,1792,4096]{2,1,0:T(8,128)(2,1)} custom-call(bf16[6,8,128,512]{3,2,1,0:T(8,128)(2,1)} %get-tuple-element.9.first, bf16[8,8,128,512]{3,2,1,0:T(8,128)(2,1)S(1)} %get-tuple-element.10.middle, bf16[14,8,128,512]{3,2,1,0:T(8,128)(2,1)S(1)} %get-tuple-element.11.last, bf16[28,8,128,512]{3,2,1,0:T(8,128)(2,1)S(1)} %get-tuple-element.12.own), custom_call_target="tpu_custom_call" | custom-call | tf_op jit(solution)/shard_map/pallas_call | solution.py:868
